TPU v7x, 32 devices: a whole 2x2x4 slice. The times are simulated.
32 devices in a mesh: gx: 4 (over x, core), gy: 4 (over z), gz: 2 (over y).
Axes of the slice: x: 2, y: 2, z: 4, core: 2. Of those that a mesh axis runs over, the one named last changes fastest.
Arguments:
- orbitals: float32 [16, 32, 32, 512], P(None, 'gx', 'gy', 'gz'), may hold values from -10 to 10
- potential: float32 [32, 32, 512], P('gx', 'gy', 'gz'), may hold values from 0 to 12
Outputs:
- updated: float32 [16, 32, 32, 512], P(None, 'gx', 'gy', 'gz')
- trial_energies: float32 [16], replicated
All inputs are finite; a program needn't handle non-finite values.
Results may differ from a plain program's by a relative error of at most 0.000022.
Values sent between devices are 32-bit elements; how exact they have to be, the bound alone decides.
A program may use at most 64 MiB of HBM per device.

v0:
```python
import jax
import jax.numpy as jnp
from jax import lax
from jax.sharding import PartitionSpec as P

COARSE_SWEEPS = 4


CENTRE_COEF = -2.5
NEAR_COEF = 4.0 / 3.0
FAR_COEF = -1.0 / 12.0
WEIGHT = 0.8
FINE_DIAG = 4.0
COARSE_DIAG = 1.75
EPSILON = 1e-06


def with_halo(block, sides, width):
    for axis, dim in sides:
        count = lax.axis_size(axis)
        forward = [(i, i + 1) for i in range(count - 1)]
        forward.append((count - 1, 0))
        backward = [(target, source) for source, target in forward]
        low = lax.ppermute(
            lax.slice_in_dim(block, block.shape[dim] - width, None, axis=dim), axis, forward
        )
        high = lax.ppermute(lax.slice_in_dim(block, 0, width, axis=dim), axis, backward)
        block = jnp.concatenate([low, block, high], axis=dim)
    return block


def neighbor(padded, margin, dimension, offset, extent):
    starts = [0, margin, margin, margin]
    starts[dimension] = margin + offset
    limits = [opening + length for opening, length in zip(starts, extent)]
    return lax.slice(padded, starts, limits)


def hamiltonian(values, potential):
    padded = with_halo(values, (("gx", 1), ("gy", 2), ("gz", 3)), 2)
    summed = 3.0 * CENTRE_COEF * values
    for dimension in (1, 2, 3):
        summed = summed + NEAR_COEF * (
            neighbor(padded, 2, dimension, -1, values.shape)
            + neighbor(padded, 2, dimension, 1, values.shape)
        )
        summed = summed + FAR_COEF * (
            neighbor(padded, 2, dimension, -2, values.shape)
            + neighbor(padded, 2, dimension, 2, values.shape)
        )
    return -0.5 * summed + potential[None] * values


def around_cells(padded, extent):
    beside_all = jnp.zeros(extent, jnp.float32)
    for dimension in (1, 2, 3):
        beside_all = (
            beside_all
            + neighbor(padded, 1, dimension, -1, extent)
            + neighbor(padded, 1, dimension, 1, extent)
        )
    return beside_all


def fine_operator(values):
    padded = with_halo(values, (("gx", 1), ("gy", 2), ("gz", 3)), 1)
    return FINE_DIAG * values - 0.5 * around_cells(padded, values.shape)


def coarse_operator(values):
    padded = with_halo(values, (("gx", 1), ("gy", 2), ("gz", 3)), 1)
    return COARSE_DIAG * values - 0.125 * around_cells(padded, values.shape)


def precondition(residual):
    smoothed = WEIGHT * residual / FINE_DIAG
    remainder = residual - fine_operator(smoothed)
    bands, size_x, size_y, size_z = remainder.shape
    blocked = (bands, size_x // 2, 2, size_y // 2, 2, size_z // 2, 2)
    coarse_res = remainder.reshape(blocked).mean(axis=(2, 4, 6))
    approx = WEIGHT * coarse_res / COARSE_DIAG
    for sweep_index in range(COARSE_SWEEPS - 1):
        approx = approx + WEIGHT * (coarse_res - coarse_operator(approx)) / COARSE_DIAG
    lifted = jnp.broadcast_to(approx[:, :, None, :, None, :, None], blocked).reshape(
        remainder.shape
    )
    second = smoothed + lifted
    return second + WEIGHT * (residual - fine_operator(second)) / FINE_DIAG


def inner_product(left, right):
    return jnp.sum(left * right, axis=(1, 2, 3))


def expand(vector):
    return vector[:, None, None, None]


def body(orbitals, potential):
    applied = hamiltonian(orbitals, potential)
    first_sums = lax.psum(
        jnp.stack([inner_product(orbitals, orbitals), inner_product(orbitals, applied)]),
        ("gx", "gy", "gz"),
    )
    norm_orbitals = first_sums[0]
    energy = first_sums[1] / (norm_orbitals + EPSILON)
    residual = applied - expand(energy) * orbitals
    corrected = precondition(residual)
    applied_corr = hamiltonian(corrected, potential)
    response = applied_corr - expand(energy) * corrected
    correlations = lax.psum(
        jnp.stack(
            [
                inner_product(residual, response),
                inner_product(response, response),
                inner_product(orbitals, corrected),
                inner_product(corrected, corrected),
                inner_product(orbitals, applied_corr),
                inner_product(corrected, applied),
                inner_product(corrected, applied_corr),
                inner_product(residual, orbitals),
                inner_product(residual, corrected),
                inner_product(response, orbitals),
                inner_product(response, corrected),
            ]
        ),
        ("gx", "gy", "gz"),
    )
    lambda_step = -correlations[0] / (correlations[1] + EPSILON)
    trial_norm = (
        norm_orbitals
        + 2.0 * lambda_step * correlations[2]
        + lambda_step * lambda_step * correlations[3]
    )
    trial_sum = (
        first_sums[1]
        + lambda_step * (correlations[4] + correlations[5])
        + lambda_step * lambda_step * correlations[6]
    )
    trial_energies = trial_sum / (trial_norm + EPSILON)
    change = trial_energies - energy
    trial_wave = orbitals + expand(lambda_step) * corrected
    residual_change = expand(lambda_step) * response - expand(change) * trial_wave
    projected = lambda_step * correlations[0] - change * (
        correlations[7] + lambda_step * correlations[8]
    )
    cross_term = correlations[9] + lambda_step * correlations[10]
    change_norm = (
        lambda_step * lambda_step * correlations[1]
        - 2.0 * lambda_step * change * cross_term
        + change * change * trial_norm
    )
    mixing_coef = -projected / (change_norm + EPSILON)
    mixed_res = residual + expand(mixing_coef) * residual_change
    updated = (
        orbitals
        + expand(mixing_coef * lambda_step) * corrected
        + expand(lambda_step) * precondition(mixed_res)
    )
    return (updated, trial_energies)


def solution(mesh):
    return jax.shard_map(
        body,
        mesh=mesh,
        in_specs=(P(None, "gx", "gy", "gz"), P("gx", "gy", "gz")),
        out_specs=(P(None, "gx", "gy", "gz"), P()),
        check_vma=False,
    )
```

profile of v0, /device:TPU:0, one launch (start us, length us, event | category | flops | bytes accessed | tf_op | source)
XLA Modules:
  0.0 567.6 jit_solution(9485600245943928243)
XLA Ops:
  15.4 9.3 %collective-permute-done.3 = f32[16,12,2,256]{3,0,2,1:T(8,128)S(1)} collective-permute-done((f32[16,12,2,256]{3,0,2,1:T(8,128)S(1)}, f32[16,12,2,256]{3,0,2,1:T(8,128)S(1)}, u32[]{:S(2)}, u32[]{:S(2)}) %collective-permute-start.3) | collective-permute-done | bytes 393248 | tf_op jit(solution)/shard_map/ppermute | solution.py:27
  25.0 8.7 %collective-permute-done.2 = f32[16,12,2,256]{3,0,2,1:T(8,128)S(1)} collective-permute-done((f32[16,12,2,256]{3,0,2,1:T(8,128)S(1)}, f32[16,12,2,256]{3,0,2,1:T(8,128)S(1)}, u32[]{:S(2)}, u32[]{:S(2)}) %collective-permute-start.2) | collective-permute-done | bytes 393248 | tf_op jit(solution)/shard_map/ppermute | solution.py:24
  53.4 7.4 %multiply_reduce_fusion.12 = (f32[16]{0:T(128)S(1)}, f32[16]{0:T(128)S(1)}, f32[16,8,8,256]{3,2,1,0:T(8,128)}) fusion(f32[16,8,8,256]{3,2,1,0:T(8,128)S(1)} %copy-done, f32[8,8,256]{2,1,0:T(8,128)S(1)} %copy-done.17, f32[16,12,12,2]{3,2,1,0:T(8,128)} %copy.716, f32[16,12,2,256]{3,2,1,0:T(2,128)S(1)} %copy.710, f32[16,12,8,256]{3,2,1,0:T(8,128)S(1)} %get-tuple-element.88, ...), kind=kLoop, calls=%fused_computation.203 | loop fusion | flops 11010016 | bytes 8753280 | tf_op jit(solution)/shard_map/reduce_sum | solution.py:92
  60.8 39.4 %psum.14 = f32[2,16]{1,0:T(2,128)S(1)} all-reduce(f32[2,16]{1,0:T(2,128)S(1)} %pad_maximum_fusion.251), channel_id=1, replica_groups=mesh['gx'=4,'gy'=4,'gz'=2] {'gx','gy','gz'}, use_global_device_ids=true, to_apply=%region_2.0 | all-reduce | flops 32 | bytes 256 | tf_op jit(solution)/shard_map/psum | solution.py:101
  109.9 4.6 collective-permute-done.9
  138.6 6.0 %copy.727 = f32[16,8,8,256]{0,3,2,1:T(8,128)} copy(f32[16,8,8,256]{3,2,1,0:T(8,128)} %fusion.53) | data formatting | bytes 2097152 | tf_op jit(solution)/shard_map/sub | solution.py:77
  144.7 8.7 %reduce_sum.137 = f32[16,4,4,128]{0,3,2,1:T(8,128)S(1)} reduce(f32[16,4,2,4,2,128,2]{0,6,5,4,3,2,1:T(2,128)} %bitcast.133, f32[]{:T(128)} %constant.50.clone.1), dimensions={2,4,6}, to_apply=%region_3.0 | reduce | flops 229376 | bytes 1179652 | tf_op jit(solution)/shard_map/reduce_sum | solution.py:80
  165.9 7.9 %collective-permute-done.16 = f32[16,6,6,1]{3,0,2,1:T(8,128)S(1)} collective-permute-done((f32[16,6,6,1]{3,0,2,1:T(8,128)S(1)}, f32[16,6,6,1]{3,0,2,1:T(8,128)S(1)}, u32[]{:S(2)}, u32[]{:S(2)}) %collective-permute-start.16) | collective-permute-done | bytes 2336 | tf_op jit(solution)/shard_map/ppermute | solution.py:24
  173.7 5.7 %collective-permute-done.17 = f32[16,6,6,1]{3,0,2,1:T(8,128)S(1)} collective-permute-done((f32[16,6,6,1]{3,0,2,1:T(8,128)S(1)}, f32[16,6,6,1]{3,0,2,1:T(8,128)S(1)}, u32[]{:S(2)}, u32[]{:S(2)}) %collective-permute-start.17) | collective-permute-done | bytes 2336 | tf_op jit(solution)/shard_map/ppermute | solution.py:27
  192.3 7.9 %collective-permute-done.22 = f32[16,6,6,1]{3,0,2,1:T(8,128)S(1)} collective-permute-done((f32[16,6,6,1]{3,0,2,1:T(8,128)S(1)}, f32[16,6,6,1]{3,0,2,1:T(8,128)S(1)}, u32[]{:S(2)}, u32[]{:S(2)}) %collective-permute-start.22) | collective-permute-done | bytes 2336 | tf_op jit(solution)/shard_map/ppermute | solution.py:24
  200.2 5.5 collective-permute-done.23
  218.0 7.9 %collective-permute-done.28 = f32[16,6,6,1]{3,0,2,1:T(8,128)S(1)} collective-permute-done((f32[16,6,6,1]{3,0,2,1:T(8,128)S(1)}, f32[16,6,6,1]{3,0,2,1:T(8,128)S(1)}, u32[]{:S(2)}, u32[]{:S(2)}) %collective-permute-start.28) | collective-permute-done | bytes 2336 | tf_op jit(solution)/shard_map/ppermute | solution.py:24
  225.8 5.2 collective-permute-done.29
  231.6 7.5 %broadcast_in_dim.4 = f32[16,4,2,4,2,128,2]{0,6,5,4,3,2,1:T(2,128)} broadcast(f32[16,4,4,128]{0,3,2,1:T(8,128)S(1)} %copy.731), dimensions={0,1,3,5} | broadcast | bytes 1179648 | tf_op jit(solution)/shard_map/broadcast_in_dim | solution.py:84
  239.0 6.1 %copy.732 = f32[16,8,8,256]{3,2,1,0:T(8,128)} copy(f32[16,8,8,256]{0,3,2,1:T(8,128)} %bitcast.134) | data formatting | bytes 2097152 | tf_op jit(solution)/shard_map/reshape | solution.py:84
  277.5 6.5 %fusion.45 = f32[16,8,8,256]{3,2,1,0:T(8,128)S(1)} fusion(f32[16,8,8,256]{3,2,1,0:T(8,128)} %copy-done.1, f32[16,8,8,256]{3,2,1,0:T(8,128)S(1)} %get-tuple-element.32, f32[16,10,10,1]{3,2,1,0:T(8,128)} %copy.742, f32[16,10,1,256]{3,2,1,0:T(1,128)S(1)} %copy.736, f32[16,10,1,256]{3,2,1,0:T(1,128)S(1)} %copy.734, f32[16,1,8,256]{3,2,1,0:T(8,128)} %copy-done.16, ...), kind=kLoop, calls=%fused_computation.112 | loop fusion | flops 7602176 | bytes 3748352 | tf_op jit(solution)/shard_map/add | solution.py:88
  285.8 5.3 collective-permute-done.36
  294.3 9.6 %collective-permute-done.39 = f32[16,12,2,256]{3,0,2,1:T(8,128)S(1)} collective-permute-done((f32[16,12,2,256]{3,0,2,1:T(8,128)S(1)}, f32[16,12,2,256]{3,0,2,1:T(8,128)S(1)}, u32[]{:S(2)}, u32[]{:S(2)}) %collective-permute-start.39) | collective-permute-done | bytes 393248 | tf_op jit(solution)/shard_map/ppermute | solution.py:27
  304.1 8.1 %collective-permute-done.38 = f32[16,12,2,256]{3,0,2,1:T(8,128)S(1)} collective-permute-done((f32[16,12,2,256]{3,0,2,1:T(8,128)S(1)}, f32[16,12,2,256]{3,0,2,1:T(8,128)S(1)}, u32[]{:S(2)}, u32[]{:S(2)}) %collective-permute-start.38) | collective-permute-done | bytes 393248 | tf_op jit(solution)/shard_map/ppermute | solution.py:24
  332.2 8.3 %multiply_reduce_fusion = (f32[16]{0:T(128)S(1)}, f32[16]{0:T(128)S(1)}, f32[16]{0:T(128)}, f32[16]{0:T(128)}, f32[16]{0:T(128)}, /*index=5*/f32[16]{0:T(128)}, ...) fusion(f32[16,8,8,256]{3,2,1,0:T(8,128)S(1)} %fusion.45, ...), kind=kLoop, calls=%fused_computation.189 | loop fusion | flops 21495632 | bytes 6656768 | tf_op jit(solution)/shard_map/reduce_sum | solution.py:92
  341.9 39.6 %psum.15 = f32[11,16]{1,0:T(8,128)S(1)} all-reduce(f32[11,16]{1,0:T(8,128)S(1)} %stack.59), channel_id=1, replica_groups=mesh['gx'=4,'gy'=4,'gz'=2] {'gx','gy','gz'}, use_global_device_ids=true, to_apply=%region_15.0 | all-reduce | flops 176 | bytes 1408 | tf_op jit(solution)/shard_map/psum | solution.py:111
  422.2 6.0 %copy.763 = f32[16,8,8,256]{0,3,2,1:T(8,128)} copy(f32[16,8,8,256]{3,2,1,0:T(8,128)} %fusion.27) | data formatting | bytes 2097152 | tf_op jit(solution)/shard_map/sub | solution.py:77
  428.2 8.7 %reduce_sum.149 = f32[16,4,4,128]{0,3,2,1:T(8,128)S(1)} reduce(f32[16,4,2,4,2,128,2]{0,6,5,4,3,2,1:T(2,128)} %bitcast.132, f32[]{:T(128)} %constant.50.clone.1), dimensions={2,4,6}, to_apply=%region_16.0 | reduce | flops 229376 | bytes 1179652 | tf_op jit(solution)/shard_map/reduce_sum | solution.py:80
  449.8 7.9 %collective-permute-done.52 = f32[16,6,6,1]{3,0,2,1:T(8,128)S(1)} collective-permute-done((f32[16,6,6,1]{3,0,2,1:T(8,128)S(1)}, f32[16,6,6,1]{3,0,2,1:T(8,128)S(1)}, u32[]{:S(2)}, u32[]{:S(2)}) %collective-permute-start.52) | collective-permute-done | bytes 2336 | tf_op jit(solution)/shard_map/ppermute | solution.py:24
  457.7 5.5 collective-permute-done.53
  475.4 7.9 %collective-permute-done.58 = f32[16,6,6,1]{3,0,2,1:T(8,128)S(1)} collective-permute-done((f32[16,6,6,1]{3,0,2,1:T(8,128)S(1)}, f32[16,6,6,1]{3,0,2,1:T(8,128)S(1)}, u32[]{:S(2)}, u32[]{:S(2)}) %collective-permute-start.58) | collective-permute-done | bytes 2336 | tf_op jit(solution)/shard_map/ppermute | solution.py:24
  483.3 5.2 collective-permute-done.59
  501.5 7.9 %collective-permute-done.64 = f32[16,6,6,1]{3,0,2,1:T(8,128)S(1)} collective-permute-done((f32[16,6,6,1]{3,0,2,1:T(8,128)S(1)}, f32[16,6,6,1]{3,0,2,1:T(8,128)S(1)}, u32[]{:S(2)}, u32[]{:S(2)}) %collective-permute-start.64) | collective-permute-done | bytes 2336 | tf_op jit(solution)/shard_map/ppermute | solution.py:24
  509.4 5.2 collective-permute-done.65
  515.1 7.5 %broadcast_in_dim.5 = f32[16,4,2,4,2,128,2]{0,6,5,4,3,2,1:T(2,128)} broadcast(f32[16,4,4,128]{0,3,2,1:T(8,128)S(1)} %copy.767), dimensions={0,1,3,5} | broadcast | bytes 1179648 | tf_op jit(solution)/shard_map/broadcast_in_dim | solution.py:84
  522.5 6.1 %copy.768 = f32[16,8,8,256]{3,2,1,0:T(8,128)} copy(f32[16,8,8,256]{0,3,2,1:T(8,128)} %bitcast.135) | data formatting | bytes 2097152 | tf_op jit(solution)/shard_map/reshape | solution.py:84
  539.0 4.6 collective-permute-done.69
  (283 shorter events, 278.5 us)
Async XLA Ops:
  1.8 6.7 %collective-permute-start = (f32[16,2,8,256]{3,2,1,0:T(8,128)S(1)}, f32[16,2,8,256]{3,2,1,0:T(8,128)S(1)}, u32[]{:S(2)}, u32[]{:S(2)}) collective-permute-start(f32[16,2,8,256]{3,2,1,0:T(8,128)S(1)} %get-tuple-element.72), channel_id=1, source_target_pairs={{0,8},{8,16},{16,24},{24,0},{1,9},{9,17},{17,25},{25,1},{2,10},{10... | collective-permute-start | bytes 786440 | tf_op jit(solution)/shard_map/ppermute | solution.py:24
  2.3 8.6 %collective-permute-start.1 = (f32[16,2,8,256]{3,2,1,0:T(8,128)S(1)}, f32[16,2,8,256]{3,2,1,0:T(8,128)S(1)}, u32[]{:S(2)}, u32[]{:S(2)}) collective-permute-start(f32[16,2,8,256]{3,2,1,0:T(8,128)S(1)} %get-tuple-element.71), channel_id=1, source_target_pairs={{8,0},{16,8},{24,16},{0,24},{9,1},{17,9},{25,17},{1,25},{10,2},{18... | collective-permute-start | bytes 786440 | tf_op jit(solution)/shard_map/ppermute | solution.py:27
  11.4 13.3 %collective-permute-start.3 = (f32[16,12,2,256]{3,0,2,1:T(8,128)S(1)}, f32[16,12,2,256]{3,0,2,1:T(8,128)S(1)}, u32[]{:S(2)}, u32[]{:S(2)}) collective-permute-start(f32[16,12,2,256]{3,0,2,1:T(8,128)S(1)} %copy.780), channel_id=1, source_target_pairs={{2,0},{4,2},{6,4},{0,6},{3,1},{5,3},{7,5},{1,7},{10,8},{12,10},{14... | collective-permute-start | bytes 1179656 | tf_op jit(solution)/shard_map/ppermute | solution.py:27
  15.3 18.4 %collective-permute-start.2 = (f32[16,12,2,256]{3,0,2,1:T(8,128)S(1)}, f32[16,12,2,256]{3,0,2,1:T(8,128)S(1)}, u32[]{:S(2)}, u32[]{:S(2)}) collective-permute-start(f32[16,12,2,256]{3,0,2,1:T(8,128)S(1)} %copy.779), channel_id=1, source_target_pairs={{0,2},{2,4},{4,6},{6,0},{1,3},{3,5},{5,7},{7,1},{8,10},{10,12},{12... | collective-permute-start | bytes 1179656 | tf_op jit(solution)/shard_map/ppermute | solution.py:24
  107.6 6.9 %collective-permute-start.9 = (f32[16,10,1,256]{3,0,2,1:T(8,128)S(1)}, f32[16,10,1,256]{3,0,2,1:T(8,128)S(1)}, u32[]{:S(2)}, u32[]{:S(2)}) collective-permute-start(f32[16,10,1,256]{3,0,2,1:T(8,128)S(1)} %copy.719), channel_id=1, source_target_pairs={{2,0},{4,2},{6,4},{0,6},{3,1},{5,3},{7,5},{1,7},{10,8},{12,10},{14... | collective-permute-start | bytes 491528 | tf_op jit(solution)/shard_map/ppermute | solution.py:27
  109.2 9.4 %collective-permute-start.8 = (f32[16,10,1,256]{3,0,2,1:T(8,128)S(1)}, f32[16,10,1,256]{3,0,2,1:T(8,128)S(1)}, u32[]{:S(2)}, u32[]{:S(2)}) collective-permute-start(f32[16,10,1,256]{3,0,2,1:T(8,128)S(1)} %copy.717), channel_id=1, source_target_pairs={{0,2},{2,4},{4,6},{6,0},{1,3},{3,5},{5,7},{7,1},{8,10},{10,12},{12... | collective-permute-start | bytes 491528 | tf_op jit(solution)/shard_map/ppermute | solution.py:24
  163.8 9.9 %collective-permute-start.16 = (f32[16,6,6,1]{3,0,2,1:T(8,128)S(1)}, f32[16,6,6,1]{3,0,2,1:T(8,128)S(1)}, u32[]{:S(2)}, u32[]{:S(2)}) collective-permute-start(f32[16,6,6,1]{3,0,2,1:T(8,128)S(1)} %get-tuple-element.83), channel_id=1, source_target_pairs={{0,1},{1,0},{2,3},{3,2},{4,5},{5,4},{6,7},{7,6},{8,9},{9,8},{10,11... | collective-permute-start | bytes 6920 | tf_op jit(solution)/shard_map/ppermute | solution.py:24
  164.2 15.3 %collective-permute-start.17 = (f32[16,6,6,1]{3,0,2,1:T(8,128)S(1)}, f32[16,6,6,1]{3,0,2,1:T(8,128)S(1)}, u32[]{:S(2)}, u32[]{:S(2)}) collective-permute-start(f32[16,6,6,1]{3,0,2,1:T(8,128)S(1)} %get-tuple-element.84), channel_id=1, source_target_pairs={{1,0},{0,1},{3,2},{2,3},{5,4},{4,5},{7,6},{6,7},{9,8},{8,9},{11,10... | collective-permute-start | bytes 6920 | tf_op jit(solution)/shard_map/ppermute | solution.py:27
  190.2 9.9 %collective-permute-start.22 = (f32[16,6,6,1]{3,0,2,1:T(8,128)S(1)}, f32[16,6,6,1]{3,0,2,1:T(8,128)S(1)}, u32[]{:S(2)}, u32[]{:S(2)}) collective-permute-start(f32[16,6,6,1]{3,0,2,1:T(8,128)S(1)} %get-tuple-element.81), channel_id=1, source_target_pairs={{0,1},{1,0},{2,3},{3,2},{4,5},{5,4},{6,7},{7,6},{8,9},{9,8},{10,11... | collective-permute-start | bytes 6920 | tf_op jit(solution)/shard_map/ppermute | solution.py:24
  191.1 14.6 %collective-permute-start.23 = (f32[16,6,6,1]{3,0,2,1:T(8,128)S(1)}, f32[16,6,6,1]{3,0,2,1:T(8,128)S(1)}, u32[]{:S(2)}, u32[]{:S(2)}) collective-permute-start(f32[16,6,6,1]{3,0,2,1:T(8,128)S(1)} %get-tuple-element.82), channel_id=1, source_target_pairs={{1,0},{0,1},{3,2},{2,3},{5,4},{4,5},{7,6},{6,7},{9,8},{8,9},{11,10... | collective-permute-start | bytes 6920 | tf_op jit(solution)/shard_map/ppermute | solution.py:27
  209.2 6.5 %collective-permute-start.26 = (f32[16,6,1,128]{3,0,2,1:T(8,128)S(1)}, f32[16,6,1,128]{3,0,2,1:T(8,128)S(1)}, u32[]{:S(2)}, u32[]{:S(2)}) collective-permute-start(f32[16,6,1,128]{3,0,2,1:T(8,128)S(1)} %get-tuple-element.95), channel_id=1, source_target_pairs={{0,2},{2,4},{4,6},{6,0},{1,3},{3,5},{5,7},{7,1},{8,10},{10,12},{12... | collective-permute-start | bytes 147464 | tf_op jit(solution)/shard_map/ppermute | solution.py:24
  215.9 9.9 %collective-permute-start.28 = (f32[16,6,6,1]{3,0,2,1:T(8,128)S(1)}, f32[16,6,6,1]{3,0,2,1:T(8,128)S(1)}, u32[]{:S(2)}, u32[]{:S(2)}) collective-permute-start(f32[16,6,6,1]{3,0,2,1:T(8,128)S(1)} %get-tuple-element.79), channel_id=1, source_target_pairs={{0,1},{1,0},{2,3},{3,2},{4,5},{5,4},{6,7},{7,6},{8,9},{9,8},{10,11... | collective-permute-start | bytes 6920 | tf_op jit(solution)/shard_map/ppermute | solution.py:24
  216.7 14.3 %collective-permute-start.29 = (f32[16,6,6,1]{3,0,2,1:T(8,128)S(1)}, f32[16,6,6,1]{3,0,2,1:T(8,128)S(1)}, u32[]{:S(2)}, u32[]{:S(2)}) collective-permute-start(f32[16,6,6,1]{3,0,2,1:T(8,128)S(1)} %get-tuple-element.80), channel_id=1, source_target_pairs={{1,0},{0,1},{3,2},{2,3},{5,4},{4,5},{7,6},{6,7},{9,8},{8,9},{11,10... | collective-permute-start | bytes 6920 | tf_op jit(solution)/shard_map/ppermute | solution.py:27
  251.5 7.7 %collective-permute-start.33 = (f32[16,10,1,256]{3,0,2,1:T(8,128)S(1)}, f32[16,10,1,256]{3,0,2,1:T(8,128)S(1)}, u32[]{:S(2)}, u32[]{:S(2)}) collective-permute-start(f32[16,10,1,256]{3,0,2,1:T(8,128)S(1)} %copy.735), channel_id=1, source_target_pairs={{2,0},{4,2},{6,4},{0,6},{3,1},{5,3},{7,5},{1,7},{10,8},{12,10},{14... | collective-permute-start | bytes 491528 | tf_op jit(solution)/shard_map/ppermute | solution.py:27
  254.8 8.9 %collective-permute-start.32 = (f32[16,10,1,256]{3,0,2,1:T(8,128)S(1)}, f32[16,10,1,256]{3,0,2,1:T(8,128)S(1)}, u32[]{:S(2)}, u32[]{:S(2)}) collective-permute-start(f32[16,10,1,256]{3,0,2,1:T(8,128)S(1)} %copy.733), channel_id=1, source_target_pairs={{0,2},{2,4},{4,6},{6,0},{1,3},{3,5},{5,7},{7,1},{8,10},{10,12},{12... | collective-permute-start | bytes 491528 | tf_op jit(solution)/shard_map/ppermute | solution.py:24
  284.0 7.1 %collective-permute-start.36 = (f32[16,2,8,256]{3,2,1,0:T(8,128)S(1)}, f32[16,2,8,256]{3,2,1,0:T(8,128)S(1)}, u32[]{:S(2)}, u32[]{:S(2)}) collective-permute-start(f32[16,2,8,256]{3,2,1,0:T(8,128)S(1)} %get-tuple-element.62), channel_id=1, source_target_pairs={{0,8},{8,16},{16,24},{24,0},{1,9},{9,17},{17,25},{25,1},{2,10},{10... | collective-permute-start | bytes 786440 | tf_op jit(solution)/shard_map/ppermute | solution.py:24
  284.1 7.3 %collective-permute-start.37 = (f32[16,2,8,256]{3,2,1,0:T(8,128)S(1)}, f32[16,2,8,256]{3,2,1,0:T(8,128)S(1)}, u32[]{:S(2)}, u32[]{:S(2)}) collective-permute-start(f32[16,2,8,256]{3,2,1,0:T(8,128)S(1)} %get-tuple-element.63), channel_id=1, source_target_pairs={{8,0},{16,8},{24,16},{0,24},{9,1},{17,9},{25,17},{1,25},{10,2},{18... | collective-permute-start | bytes 786440 | tf_op jit(solution)/shard_map/ppermute | solution.py:27
  291.8 12.0 %collective-permute-start.39 = (f32[16,12,2,256]{3,0,2,1:T(8,128)S(1)}, f32[16,12,2,256]{3,0,2,1:T(8,128)S(1)}, u32[]{:S(2)}, u32[]{:S(2)}) collective-permute-start(f32[16,12,2,256]{3,0,2,1:T(8,128)S(1)} %copy.745), channel_id=1, source_target_pairs={{2,0},{4,2},{6,4},{0,6},{3,1},{5,3},{7,5},{1,7},{10,8},{12,10},{14... | collective-permute-start | bytes 1179656 | tf_op jit(solution)/shard_map/ppermute | solution.py:27
  293.9 18.3 %collective-permute-start.38 = (f32[16,12,2,256]{3,0,2,1:T(8,128)S(1)}, f32[16,12,2,256]{3,0,2,1:T(8,128)S(1)}, u32[]{:S(2)}, u32[]{:S(2)}) collective-permute-start(f32[16,12,2,256]{3,0,2,1:T(8,128)S(1)} %copy.743), channel_id=1, source_target_pairs={{0,2},{2,4},{4,6},{6,0},{1,3},{3,5},{5,7},{7,1},{8,10},{10,12},{12... | collective-permute-start | bytes 1179656 | tf_op jit(solution)/shard_map/ppermute | solution.py:24
  318.5 6.4 %collective-permute-start.40 = (f32[16,12,12,2]{0,3,2,1:T(2,128)}, f32[16,12,12,2]{0,3,2,1:T(2,128)}, u32[]{:S(2)}, u32[]{:S(2)}) collective-permute-start(f32[16,12,12,2]{0,3,2,1:T(2,128)} %copy.749), channel_id=1, source_target_pairs={{0,1},{1,0},{2,3},{3,2},{4,5},{5,4},{6,7},{7,6},{8,9},{9,8},{10,11... | collective-permute-start | bytes 55304 | tf_op jit(solution)/shard_map/ppermute | solution.py:24
  390.5 6.9 %collective-permute-start.45 = (f32[16,10,1,256]{3,0,2,1:T(8,128)S(1)}, f32[16,10,1,256]{3,0,2,1:T(8,128)S(1)}, u32[]{:S(2)}, u32[]{:S(2)}) collective-permute-start(f32[16,10,1,256]{3,0,2,1:T(8,128)S(1)} %copy.755), channel_id=1, source_target_pairs={{2,0},{4,2},{6,4},{0,6},{3,1},{5,3},{7,5},{1,7},{10,8},{12,10},{14... | collective-permute-start | bytes 491528 | tf_op jit(solution)/shard_map/ppermute | solution.py:27
  392.9 9.1 %collective-permute-start.44 = (f32[16,10,1,256]{3,0,2,1:T(8,128)S(1)}, f32[16,10,1,256]{3,0,2,1:T(8,128)S(1)}, u32[]{:S(2)}, u32[]{:S(2)}) collective-permute-start(f32[16,10,1,256]{3,0,2,1:T(8,128)S(1)} %copy.753), channel_id=1, source_target_pairs={{0,2},{2,4},{4,6},{6,0},{1,3},{3,5},{5,7},{7,1},{8,10},{10,12},{12... | collective-permute-start | bytes 491528 | tf_op jit(solution)/shard_map/ppermute | solution.py:24
  447.7 9.9 %collective-permute-start.52 = (f32[16,6,6,1]{3,0,2,1:T(8,128)S(1)}, f32[16,6,6,1]{3,0,2,1:T(8,128)S(1)}, u32[]{:S(2)}, u32[]{:S(2)}) collective-permute-start(f32[16,6,6,1]{3,0,2,1:T(8,128)S(1)} %get-tuple-element.77), channel_id=1, source_target_pairs={{0,1},{1,0},{2,3},{3,2},{4,5},{5,4},{6,7},{7,6},{8,9},{9,8},{10,11... | collective-permute-start | bytes 6920 | tf_op jit(solution)/shard_map/ppermute | solution.py:24
  448.2 15.0 %collective-permute-start.53 = (f32[16,6,6,1]{3,0,2,1:T(8,128)S(1)}, f32[16,6,6,1]{3,0,2,1:T(8,128)S(1)}, u32[]{:S(2)}, u32[]{:S(2)}) collective-permute-start(f32[16,6,6,1]{3,0,2,1:T(8,128)S(1)} %get-tuple-element.78), channel_id=1, source_target_pairs={{1,0},{0,1},{3,2},{2,3},{5,4},{4,5},{7,6},{6,7},{9,8},{8,9},{11,10... | collective-permute-start | bytes 6920 | tf_op jit(solution)/shard_map/ppermute | solution.py:27
  466.8 6.4 %collective-permute-start.56 = (f32[16,6,1,128]{3,0,2,1:T(8,128)S(1)}, f32[16,6,1,128]{3,0,2,1:T(8,128)S(1)}, u32[]{:S(2)}, u32[]{:S(2)}) collective-permute-start(f32[16,6,1,128]{3,0,2,1:T(8,128)S(1)} %get-tuple-element.91), channel_id=1, source_target_pairs={{0,2},{2,4},{4,6},{6,0},{1,3},{3,5},{5,7},{7,1},{8,10},{10,12},{12... | collective-permute-start | bytes 147464 | tf_op jit(solution)/shard_map/ppermute | solution.py:24
  473.4 9.9 %collective-permute-start.58 = (f32[16,6,6,1]{3,0,2,1:T(8,128)S(1)}, f32[16,6,6,1]{3,0,2,1:T(8,128)S(1)}, u32[]{:S(2)}, u32[]{:S(2)}) collective-permute-start(f32[16,6,6,1]{3,0,2,1:T(8,128)S(1)} %get-tuple-element.75), channel_id=1, source_target_pairs={{0,1},{1,0},{2,3},{3,2},{4,5},{5,4},{6,7},{7,6},{8,9},{9,8},{10,11... | collective-permute-start | bytes 6920 | tf_op jit(solution)/shard_map/ppermute | solution.py:24
  473.9 14.6 %collective-permute-start.59 = (f32[16,6,6,1]{3,0,2,1:T(8,128)S(1)}, f32[16,6,6,1]{3,0,2,1:T(8,128)S(1)}, u32[]{:S(2)}, u32[]{:S(2)}) collective-permute-start(f32[16,6,6,1]{3,0,2,1:T(8,128)S(1)} %get-tuple-element.76), channel_id=1, source_target_pairs={{1,0},{0,1},{3,2},{2,3},{5,4},{4,5},{7,6},{6,7},{9,8},{8,9},{11,10... | collective-permute-start | bytes 6920 | tf_op jit(solution)/shard_map/ppermute | solution.py:27
  492.1 6.2 %collective-permute-start.62 = (f32[16,6,1,128]{3,0,2,1:T(8,128)S(1)}, f32[16,6,1,128]{3,0,2,1:T(8,128)S(1)}, u32[]{:S(2)}, u32[]{:S(2)}) collective-permute-start(f32[16,6,1,128]{3,0,2,1:T(8,128)S(1)} %get-tuple-element.89), channel_id=1, source_target_pairs={{0,2},{2,4},{4,6},{6,0},{1,3},{3,5},{5,7},{7,1},{8,10},{10,12},{12... | collective-permute-start | bytes 147464 | tf_op jit(solution)/shard_map/ppermute | solution.py:24
  499.4 9.9 %collective-permute-start.64 = (f32[16,6,6,1]{3,0,2,1:T(8,128)S(1)}, f32[16,6,6,1]{3,0,2,1:T(8,128)S(1)}, u32[]{:S(2)}, u32[]{:S(2)}) collective-permute-start(f32[16,6,6,1]{3,0,2,1:T(8,128)S(1)} %get-tuple-element.73), channel_id=1, source_target_pairs={{0,1},{1,0},{2,3},{3,2},{4,5},{5,4},{6,7},{7,6},{8,9},{9,8},{10,11... | collective-permute-start | bytes 6920 | tf_op jit(solution)/shard_map/ppermute | solution.py:24
  499.8 14.7 %collective-permute-start.65 = (f32[16,6,6,1]{3,0,2,1:T(8,128)S(1)}, f32[16,6,6,1]{3,0,2,1:T(8,128)S(1)}, u32[]{:S(2)}, u32[]{:S(2)}) collective-permute-start(f32[16,6,6,1]{3,0,2,1:T(8,128)S(1)} %get-tuple-element.74), channel_id=1, source_target_pairs={{1,0},{0,1},{3,2},{2,3},{5,4},{4,5},{7,6},{6,7},{9,8},{8,9},{11,10... | collective-permute-start | bytes 6920 | tf_op jit(solution)/shard_map/ppermute | solution.py:27
  535.3 8.2 %collective-permute-start.69 = (f32[16,10,1,256]{3,0,2,1:T(8,128)S(1)}, f32[16,10,1,256]{3,0,2,1:T(8,128)S(1)}, u32[]{:S(2)}, u32[]{:S(2)}) collective-permute-start(f32[16,10,1,256]{3,0,2,1:T(8,128)S(1)} %copy.771), channel_id=1, source_target_pairs={{2,0},{4,2},{6,4},{0,6},{3,1},{5,3},{7,5},{1,7},{10,8},{12,10},{14... | collective-permute-start | bytes 491528 | tf_op jit(solution)/shard_map/ppermute | solution.py:27
  538.9 8.6 %collective-permute-start.68 = (f32[16,10,1,256]{3,0,2,1:T(8,128)S(1)}, f32[16,10,1,256]{3,0,2,1:T(8,128)S(1)}, u32[]{:S(2)}, u32[]{:S(2)}) collective-permute-start(f32[16,10,1,256]{3,0,2,1:T(8,128)S(1)} %copy.769), channel_id=1, source_target_pairs={{0,2},{2,4},{4,6},{6,0},{1,3},{3,5},{5,7},{7,1},{8,10},{10,12},{12... | collective-permute-start | bytes 491528 | tf_op jit(solution)/shard_map/ppermute | solution.py:24
  (58 other events, 394.5 us)
where the time goes:
time: 576 us; the launch traced here: 568 us
  waiting for transfers between devices  207 us (36%)
  local copies, waits for them, and re-layouts  125 us (22%)
  starting transfers between devices  89 us (15%)
  blocking collectives  79 us (14%)
  other arithmetic  65.7 us (11%)
    ppermute x36, waiting for transfers between devices, with_halo(): lax.ppermute(lax.slice_in_dim(block, block.shape[dim] - width, None, axis...  126 us
    ppermute x36, waiting for transfers between devices, with_halo(): lax.ppermute(lax.slice_in_dim(block, 0, width, axis=dim), axis, backward)  80.3 us
    ppermute x36, starting transfers between devices, with_halo(): lax.ppermute(lax.slice_in_dim(block, 0, width, axis=dim), axis, backward)  69.4 us
    psum x1, blocking collectives, body(): lax.psum(jnp.stack([inner_product(residual, response), inner_product(resp...  39.6 us
    psum x1, blocking collectives, body(): lax.psum(jnp.stack([inner_product(orbitals, orbitals), inner_product(orbi...  39.4 us
    slice x35, local copies, waits for them, and re-layouts, with_halo(): lax.slice_in_dim(block, block.shape[dim] - width, None, axis=dim)  27.5 us
    ppermute x36, starting transfers between devices, with_halo(): lax.ppermute(lax.slice_in_dim(block, block.shape[dim] - width, None, axis...  19.7 us
    ppermute x12, local copies, waits for them, and re-layouts, with_halo(): lax.ppermute(lax.slice_in_dim(block, 0, width, axis=dim), axis, backward)  19.1 us
  transfers between devices with their start and end apart: 72, of which 59 were waited for; matrix products, arithmetic and copies ran while one was open for 6% of the time, Pallas kernels for 0%

commit v1 on v0

v1 whole, which is shorter than its diff:
```python
import functools

import jax
import jax.numpy as jnp
from jax import lax
from jax.experimental import pallas as pl
from jax.experimental.pallas import tpu as pltpu
from jax.sharding import PartitionSpec as P

COARSE_SWEEPS = 4
WEIGHT = 0.8
COARSE_DIAG = 1.75
EPSILON = 1e-06
LANES = 128
ROWS = 8
GROUPS = 2
AXES = ("gx", "gy", "gz")
MESH = pl.DeviceIdType.MESH
NDOTS = 8


def kernel(sizes, orb_hbm, pot, out, energies, *scratch):
    (
        orb, app, res, cor, rsp, rem, coarse,
        fys, fyr, fzs, fzr, hy, cxs, cxr, cys, cyr, czs, czr, hcy,
        acc, scal, red, load_sem, send_sem, recv_sem, rsend, rrecv,
    ) = scratch
    nx, ny, nz = sizes
    bands, xs = orb_hbm.shape[0], orb_hbm.shape[1]
    tiles = orb_hbm.shape[3] // LANES
    xc = xs // 2
    per = bands // GROUPS
    me = [lax.axis_index(a) for a in AXES]
    right = [lax.rem(m + 1, n) for m, n in zip(me, sizes)]
    left = [lax.rem(m + n - 1, n) for m, n in zip(me, sizes)]

    loads = [
        pltpu.make_async_copy(
            orb_hbm.at[:, :, :, pl.ds(t * LANES, LANES)],
            orb.at[:, pl.ds(2, xs), t],
            load_sem.at[t],
        )
        for t in range(tiles)
    ]
    for c in loads:
        c.start()
    barrier = pltpu.get_barrier_semaphore()
    for k, a in enumerate(AXES):
        for d in range(1, sizes[k]):
            pl.semaphore_signal(
                barrier, inc=1, device_id={a: lax.rem(me[k] + d, sizes[k])}, device_id_type=MESH
            )
    pl.semaphore_wait(barrier, sum(sizes) - 3)
    for c in loads:
        c.wait()

    row = lax.broadcasted_iota(jnp.int32, (ROWS, LANES), 0)
    lane = lax.broadcasted_iota(jnp.int32, (ROWS, LANES), 1)
    even_lane = lane % 2 == 0
    even_row = row % 2 == 0
    low_half = lane < LANES // 2
    first_of_four = lane % 4 < 2

    def roll(v, k, axis):
        return pltpu.roll(v, k % v.shape[axis], axis)

    def flat(ref):
        n = 1
        for s in ref.shape[:-1]:
            n *= s
        return ref.reshape(n, LANES)

    def loop(lo, hi, f):
        def step(i, carry):
            f(i)
            return carry

        lax.fori_loop(lo, hi, step, 0)

    def remote(src, dst, slot, k, axis, target):
        return pltpu.make_async_remote_copy(
            src_ref=src,
            dst_ref=dst,
            send_sem=send_sem.at[slot, k],
            recv_sem=recv_sem.at[slot, k],
            device_id={axis: target},
            device_id_type=MESH,
        )

    def z_copies(src, dst_l, dst_r, slot):
        copies = [remote(src, dst_l, slot, 4, "gz", right[2])]
        if nz > 2:
            copies.append(remote(src, dst_r, slot, 5, "gz", left[2]))
        return copies

    def fine_send(field, which, depth, g):
        lo = g * per
        view = flat(field)
        span = field.shape[1]
        ys, yr = fys[which], fyr[which]
        zs, zr = fzs[which], fzr[which]

        def pack(b):
            for t in range(tiles):
                for j in range(depth):
                    base = ((b * span + 2) * tiles + t) * ROWS
                    ys[0, b, j, t] = view[pl.ds(base + ROWS - depth + j, xs, stride=tiles * ROWS), :]
                    ys[1, b, j, t] = view[pl.ds(base + j, xs, stride=tiles * ROWS), :]
            packed = jnp.zeros((ROWS, LANES), jnp.float32)
            for x in range(xs):
                w = jnp.where(low_half, field[b, 2 + x, 0], field[b, 2 + x, tiles - 1])
                packed = jnp.where(lane // 4 == x, roll(w, 2 + 4 * x, 1), packed)
            zs[b] = packed

        loop(lo, lo + per, pack)
        slot = which * GROUPS + g
        part = pl.ds(lo, per)
        copies = [
            remote(field.at[part, pl.ds(2 + xs - depth, depth)], field.at[part, pl.ds(2 - depth, depth)], slot, 0, "gx", right[0]),
            remote(field.at[part, pl.ds(2, depth)], field.at[part, pl.ds(2 + xs, depth)], slot, 1, "gx", left[0]),
            remote(ys.at[0, part], yr.at[0, part], slot, 2, "gy", right[1]),
            remote(ys.at[1, part], yr.at[1, part], slot, 3, "gy", left[1]),
        ] + z_copies(zs.at[part], zr.at[0, part], zr.at[1, part], slot)
        for c in copies:
            c.start()
        return copies

    def wait(copies):
        for c in copies:
            c.wait()

    def z_packed(zr, b):
        if nz > 2:
            return jnp.where(first_of_four, zr[0, b], zr[1, b])
        return zr[0, b]

    def unpack_y(yr, b, depth):
        view = flat(hy)
        for t in range(tiles):
            for j in range(depth):
                base = (b * xs * tiles + t) * ROWS
                view[pl.ds(base + ROWS - depth + j, xs, stride=tiles * ROWS), :] = yr(0, j, t)
                view[pl.ds(base + j, xs, stride=tiles * ROWS), :] = yr(1, j, t)

    def shifted_y(v, h, k):
        up = roll(jnp.where(row >= ROWS - k, h, v), k, 0)
        down = roll(jnp.where(row < k, h, v), -k, 0)
        return up + down

    def shifted_z(vs, hz, k):
        before = [hz] + vs[:-1]
        after = vs[1:] + [hz]
        return [
            roll(jnp.where(lane >= LANES - k, p, v), k, 1) + roll(jnp.where(lane < k, n, v), -k, 1)
            for p, v, n in zip(before, vs, after)
        ]

    def hamiltonian(field, which, b, use):
        unpack_y(lambda s, j, t: fyr[which][s, b, j, t], b, 2)
        zp = z_packed(fzr[which], b)
        for x in range(xs):
            hz = roll(zp, -(4 * x + 2), 1)
            vs = [field[b, 2 + x, t] for t in range(tiles)]
            z1, z2 = shifted_z(vs, hz, 1), shifted_z(vs, hz, 2)
            outs = []
            for t in range(tiles):
                h = hy[b, x, t]
                near = field[b, 1 + x, t] + field[b, 3 + x, t] + shifted_y(vs[t], h, 1) + z1[t]
                far = field[b, x, t] + field[b, 4 + x, t] + shifted_y(vs[t], h, 2) + z2[t]
                potential = pot[x, :, t * LANES : (t + 1) * LANES]
                outs.append((potential + 3.75) * vs[t] - (2.0 / 3.0) * near + (1.0 / 24.0) * far)
            use(x, vs, outs)

    def rowsum(vs):
        return jnp.sum(functools.reduce(jnp.add, vs), axis=0, keepdims=True)

    def reduce_all(index, ndots):
        wide = lax.broadcasted_iota(jnp.int32, (bands, LANES), 1)
        total = jnp.zeros((bands, LANES), jnp.float32)
        for q in range(ndots):
            total = jnp.where(wide == q, jnp.sum(acc[q], axis=1, keepdims=True), total)
        for stage, k in enumerate((2, 1, 0)):
            n = sizes[k]
            buf = red.at[index * 3 + stage]
            buf[me[k]] = total
            copies = []
            for d in range(1, n):
                copies.append(
                    pltpu.make_async_remote_copy(
                        src_ref=buf.at[me[k]],
                        dst_ref=buf.at[me[k]],
                        send_sem=rsend.at[index * 3 + stage, d],
                        recv_sem=rrecv.at[index * 3 + stage, d],
                        device_id={AXES[k]: lax.rem(me[k] + d, n)},
                        device_id_type=MESH,
                    )
                )
            for c in copies:
                c.start()
            for c in copies:
                c.wait()
            total = buf[0]
            for i in range(1, n):
                total = total + buf[i]
        return [total[:, q : q + 1] for q in range(ndots)]

    def put(k, column):
        scal[k] = jnp.broadcast_to(column, (bands, LANES))

    def get(k, b):
        return scal[k, pl.ds(b, 1), :]

    def restrict(b, ry, rz):
        unpack_y(ry, b, 1)
        for X in range(xc):
            pair = [None] * tiles
            for x in (2 * X, 2 * X + 1):
                hz = roll(rz, -(4 * x + 2), 1)
                vs = [res[b, 2 + x, t] for t in range(tiles)]
                z1 = shifted_z(vs, hz, 1)
                for t in range(tiles):
                    s = res[b, 1 + x, t] + res[b, 3 + x, t] + shifted_y(vs[t], hy[b, x, t], 1) + z1[t]
                    m = (1.0 - WEIGHT) * vs[t] + (0.5 * WEIGHT / 4.0) * s
                    rem[b, x, t] = m
                    pair[t] = m if pair[t] is None else pair[t] + m
            for t in range(tiles):
                s = pair[t]
                s = s + jnp.where(even_row, roll(s, -1, 0), roll(s, 1, 0))
                s = s + jnp.where(even_lane, roll(s, -1, 1), roll(s, 1, 1))
                coarse[0, b, 1 + X, t] = s * (0.125 * WEIGHT / COARSE_DIAG)

    def coarse_send(which, level, g):
        cf = coarse.at[level]
        view = flat(coarse)
        lo = g * per // 4

        def pack(i):
            b = 4 * i
            for t in range(tiles):
                for side, X in ((0, xc), (1, 1)):
                    lanes = [
                        jnp.where(even_lane, cf[b + k, X, t], cf[b + k + 1, X, t]) for k in (0, 2)
                    ]
                    cxs[which, side, i, t] = jnp.where(even_row, lanes[0], lanes[1])
                for side, j in ((0, ROWS - 1), (1, 0)):
                    vs = [
                        view[pl.ds((((level * bands + b + k) * (xc + 2) + 1) * tiles + t) * ROWS + j, xc, stride=tiles * ROWS), :]
                        for k in range(4)
                    ]
                    ev = even_lane[:xc]
                    cys[which, side, i, t, 0:xc] = jnp.where(ev, vs[0], vs[1])
                    cys[which, side, i, t, xc : 2 * xc] = jnp.where(ev, vs[2], vs[3])

        loop(lo, lo + per // 4, pack)

        def pack_z(i):
            packed = jnp.zeros((ROWS, LANES), jnp.float32)
            for k in range(8):
                for X in range(xc):
                    off = 4 * (k * xc + X)
                    w = jnp.where(low_half, cf[8 * i + k, 1 + X, 0], cf[8 * i + k, 1 + X, tiles - 1])
                    packed = jnp.where(lane // 4 == off // 4, roll(w, 2 + off, 1), packed)
            czs[which, i] = packed

        loop(g * per // 8, (g + 1) * per // 8, pack_z)
        slot = (4 + which) * GROUPS + g
        part = pl.ds(lo, per // 4)
        zpart = pl.ds(g * per // 8, per // 8)
        copies = [
            remote(cxs.at[which, 0, part], cxr.at[which, 0, part], slot, 0, "gx", right[0]),
            remote(cxs.at[which, 1, part], cxr.at[which, 1, part], slot, 1, "gx", left[0]),
            remote(cys.at[which, 0, part], cyr.at[which, 0, part], slot, 2, "gy", right[1]),
            remote(cys.at[which, 1, part], cyr.at[which, 1, part], slot, 3, "gy", left[1]),
        ] + z_copies(czs.at[which, zpart], czr.at[which, 0, zpart], czr.at[which, 1, zpart], slot)
        for c in copies:
            c.start()
        return copies

    def spread_lanes(p):
        return (
            jnp.where(even_lane, p, roll(p, 1, 1)),
            jnp.where(even_lane, roll(p, -1, 1), p),
        )

    def coarse_unpack(which, level, g):
        cf = coarse.at[level]
        view = flat(hcy)
        lo = g * per // 4

        def unpack(i):
            b = 4 * i
            for t in range(tiles):
                for side, X in ((0, 0), (1, xc + 1)):
                    p = cxr[which, side, i, t]
                    top = jnp.where(even_row, p, roll(p, 1, 0))
                    low = jnp.where(even_row, roll(p, -1, 0), p)
                    for k, v in enumerate(spread_lanes(top) + spread_lanes(low)):
                        cf[b + k, X, t] = v
                for side, j in ((0, ROWS - 2), (1, 0)):
                    first, second = spread_lanes(cyr[which, side, i, t])
                    for k, v in enumerate((first[:xc], second[:xc], first[xc:], second[xc:])):
                        base = ((b + k) * xc * tiles + t) * ROWS + j
                        for dup in range(2):
                            view[pl.ds(base + dup, xc, stride=tiles * ROWS), :] = v

        loop(lo, lo + per // 4, unpack)

    def coarse_loop(which, g, f):
        def bundle(i):
            zp = czr[which, 0, i]
            if nz > 2:
                zp = jnp.where(first_of_four, zp, czr[which, 1, i])
            for k in range(8):
                f(8 * i + k, lambda X, k=k: roll(zp, -(4 * (k * xc + X) + 2), 1))

        loop(g * per // 8, (g + 1) * per // 8, bundle)

    def sweep(which, level, g):
        coarse_unpack(which, level, g)

        def one(b, hz):
            for X in range(xc):
                vs = [coarse[level, b, 1 + X, t] for t in range(tiles)]
                z = shifted_z(vs, hz(X), 2)
                for t in range(tiles):
                    s = coarse[level, b, X, t] + coarse[level, b, 2 + X, t] + shifted_y(vs[t], hcy[b, X, t], 2) + z[t]
                    rhs = coarse[0, b, 1 + X, t]
                    coarse[level + 1, b, 1 + X, t] = (
                        (1.0 - WEIGHT) * vs[t] + (0.125 * WEIGHT / COARSE_DIAG) * s + rhs
                    )

        coarse_loop(which, g, one)

    def prolong(which, level, g, use):
        coarse_unpack(which, level, g)

        def one(b, hz):
            for X in range(xc):
                vs = [coarse[level, b, 1 + X, t] for t in range(tiles)]
                z = shifted_z(vs, hz(X), 1)
                for t in range(tiles):
                    s = shifted_y(vs[t], hcy[b, X, t], 1) + z[t] + vs[t]
                    for x, other in ((2 * X, X), (2 * X + 1, 2 + X)):
                        total = s + coarse[level, b, other, t]
                        kr = (1.0 - WEIGHT) * (res[b, 2 + x, t] + vs[t] + rem[b, x, t]) + (
                            0.5 * WEIGHT / 4.0
                        ) * total
                        use(b, x, t, kr)

        coarse_loop(which, g, one)

    groups = range(GROUPS)

    def precondition(base, prepare, use):
        flight = []
        for g in groups:
            loop(g * per, (g + 1) * per, prepare)
            flight.append(coarse_send(base, 0, g))
        for s in range(COARSE_SWEEPS - 1):
            for g in groups:
                wait(flight[g])
                sweep(base + s, s, g)
                flight[g] = coarse_send(base + s + 1, s + 1, g)
        for g in groups:
            wait(flight[g])
            prolong(base + COARSE_SWEEPS - 1, COARSE_SWEEPS - 1, g, use)
            yield g

    flight = [fine_send(orb, 0, 2, g) for g in groups]
    second = []
    for g in groups:
        wait(flight[g])

        def apply_one(b):
            norm, energy = [], []

            def use(x, vs, outs):
                for t in range(tiles):
                    app[b, 2 + x, t] = outs[t]
                    norm.append(vs[t] * vs[t])
                    energy.append(vs[t] * outs[t])

            hamiltonian(orb, 0, b, use)
            acc[0, pl.ds(b, 1), :] = rowsum(norm)
            acc[1, pl.ds(b, 1), :] = rowsum(energy)

        loop(g * per, (g + 1) * per, apply_one)
        second.append(fine_send(app, 1, 1, g))
    norm_orbitals, first_energy = reduce_all(0, 2)
    energy = first_energy / (norm_orbitals + EPSILON)
    put(0, energy)
    for c in second:
        wait(c)

    def prepare_first(b):
        e = get(0, b)
        for x in range(1, xs + 3):
            for t in range(tiles):
                res[b, x, t] = app[b, x, t] - e * orb[b, x, t]

        def ry(s, j, t):
            return fyr[1][s, b, 0, t] - e * fyr[0][s, b, 1 - s, t]

        restrict(b, ry, z_packed(fzr[1], b) - e * z_packed(fzr[0], b))

    def use_first(b, x, t, kr):
        cor[b, 2 + x, t] = kr

    flight = []
    for g in precondition(0, prepare_first, use_first):
        flight.append(fine_send(cor, 2, 2, g))
    second = []
    for g in groups:
        wait(flight[g])

        def respond_one(b):
            e = get(0, b)
            dots = [[] for _ in range(NDOTS)]

            def use(x, vs, outs):
                for t in range(tiles):
                    c, o, r = vs[t], orb[b, 2 + x, t], res[b, 2 + x, t]
                    p = outs[t] - e * c
                    rsp[b, 2 + x, t] = p
                    for q, (u, v) in enumerate(((r, p), (p, p), (o, c), (c, c), (p, o), (p, c), (r, o), (r, c))):
                        w = u * v
                        dots[q] = [w] if not dots[q] else [dots[q][0] + w]

            hamiltonian(cor, 2, b, use)
            for q in range(NDOTS):
                acc[q, pl.ds(b, 1), :] = rowsum(dots[q])

        loop(g * per, (g + 1) * per, respond_one)
        second.append(fine_send(rsp, 3, 1, g))
    rp, pp, oc, cc, po, pc, ro, rc = reduce_all(1, NDOTS)
    lam = -rp / (pp + EPSILON)
    trial_norm = norm_orbitals + 2.0 * lam * oc + lam * lam * cc
    trial_sum = (
        first_energy + lam * ((po + energy * oc) + (rc + energy * oc)) + lam * lam * (pc + energy * cc)
    )
    trial = trial_sum / (trial_norm + EPSILON)
    energies[...] = jnp.broadcast_to(trial, (bands, LANES))
    change = trial - energy
    projected = lam * rp - change * (ro + lam * rc)
    cross = po + lam * pc
    change_norm = lam * lam * pp - 2.0 * lam * change * cross + change * change * trial_norm
    mix = -projected / (change_norm + EPSILON)
    put(1, lam)
    put(2, mix * lam)
    put(3, mix * change)
    put(4, mix * change * lam)
    for c in second:
        wait(c)

    def prepare_second(b):
        e, ml, mc, mcl = get(0, b), get(2, b), get(3, b), get(4, b)

        def mixed(r, p, o, c):
            return r + ml * p - mc * o - mcl * c

        for x in range(1, xs + 3):
            for t in range(tiles):
                res[b, x, t] = mixed(res[b, x, t], rsp[b, x, t], orb[b, x, t], cor[b, x, t])

        def ry(s, j, t):
            o = fyr[0][s, b, 1 - s, t]
            r = fyr[1][s, b, 0, t] - e * o
            return mixed(r, fyr[3][s, b, 0, t], o, fyr[2][s, b, 1 - s, t])

        oz = z_packed(fzr[0], b)
        rz = z_packed(fzr[1], b) - e * oz
        restrict(b, ry, mixed(rz, z_packed(fzr[3], b), oz, z_packed(fzr[2], b)))

    def use_second(b, x, t, kr):
        out[b, x, :, t * LANES : (t + 1) * LANES] = (
            orb[b, 2 + x, t] + get(2, b) * cor[b, 2 + x, t] + get(1, b) * kr
        )

    for g in precondition(COARSE_SWEEPS, prepare_second, use_second):
        pass


def solution(mesh):
    sizes = tuple(mesh.shape[a] for a in AXES)

    def body(orbitals, potential):
        bands, xs, ys, zs = orbitals.shape
        tiles = zs // LANES
        tile = (ROWS, LANES)
        vmem = lambda *s: pltpu.VMEM(s + tile, jnp.float32)
        field = vmem(bands, xs + 4, tiles)
        exchanges = 4 + 2 * COARSE_SWEEPS
        faces = (2 * COARSE_SWEEPS, 2, bands // 4, tiles)
        peers = max(sizes)

        def call(*refs):
            refs = list(refs)
            head, rest = refs[:4], refs[4:]
            fields, rest = rest[:7], rest[7:]
            fys, rest = rest[:4], rest[4:]
            fyr, rest = rest[:4], rest[4:]
            fzs, rest = rest[:4], rest[4:]
            fzr, rest = rest[:4], rest[4:]
            kernel(sizes, *head, *fields, fys, fyr, fzs, fzr, *rest)

        depths = (2, 1, 2, 1)
        updated, trial = pl.pallas_call(
            call,
            out_shape=(
                jax.ShapeDtypeStruct(orbitals.shape, jnp.float32),
                jax.ShapeDtypeStruct((bands, LANES), jnp.float32),
            ),
            in_specs=[
                pl.BlockSpec(memory_space=pl.ANY),
                pl.BlockSpec(memory_space=pltpu.VMEM),
            ],
            out_specs=(
                pl.BlockSpec(memory_space=pltpu.VMEM),
                pl.BlockSpec(memory_space=pltpu.VMEM),
            ),
            scratch_shapes=[field] * 5
            + [vmem(bands, xs, tiles), vmem(COARSE_SWEEPS, bands, xs // 2 + 2, tiles)]
            + [vmem(2, bands, d, tiles) for d in depths]
            + [vmem(2, bands, d, tiles) for d in depths]
            + [vmem(bands) for d in depths]
            + [vmem(2, bands) for d in depths]
            + [
                vmem(bands, xs, tiles),
                vmem(*faces),
                vmem(*faces),
                vmem(*faces),
                vmem(*faces),
                vmem(2 * COARSE_SWEEPS, bands // 8),
                vmem(2 * COARSE_SWEEPS, 2, bands // 8),
                vmem(bands, xs // 2, tiles),
                pltpu.VMEM((NDOTS, bands, LANES), jnp.float32),
                pltpu.VMEM((5, bands, LANES), jnp.float32),
                pltpu.VMEM((6, peers, bands, LANES), jnp.float32),
                pltpu.SemaphoreType.DMA((tiles,)),
                pltpu.SemaphoreType.DMA((exchanges * GROUPS, 6)),
                pltpu.SemaphoreType.DMA((exchanges * GROUPS, 6)),
                pltpu.SemaphoreType.DMA((6, peers)),
                pltpu.SemaphoreType.DMA((6, peers)),
            ],
            compiler_params=pltpu.CompilerParams(
                collective_id=0, has_side_effects=True, vmem_limit_bytes=48 * 1024 * 1024
            ),
        )(orbitals, potential)
        return updated, trial[:, 0]

    return jax.shard_map(
        body,
        mesh=mesh,
        in_specs=(P(None, "gx", "gy", "gz"), P("gx", "gy", "gz")),
        out_specs=(P(None, "gx", "gy", "gz"), P()),
        check_vma=False,
    )
```

time: 576 us -> 110 us (0.19); the launches traced: 568 us -> 109 us
  waiting for transfers between devices: 207 us -> 0 us
  local copies, waits for them, and re-layouts: 125 us -> 3.65 us
  Pallas kernels: 0 us -> 105 us
  starting transfers between devices: 89 us -> 0 us
  blocking collectives: 79 us -> 0 us
  other arithmetic: 65.7 us -> 0 us
    ppermute x72 -> x0, waiting for transfers between devices: 207 us -> none  [the longest x36 126 us: with_halo(): lax.ppermute(lax.slice_in_dim(block, block.shape[dim] - width, None, axis...]
    pallas_call x0 -> x1, Pallas kernels: none -> 105 us  [body(): pl.pallas_call(call, out_shape=(jax.ShapeDtypeStruct(orbitals.shape, jnp....]
    ppermute x72 -> x0, starting transfers between devices: 89 us -> none  [the longest x36 69.4 us: with_halo(): lax.ppermute(lax.slice_in_dim(block, 0, width, axis=dim), axis, backward)]
    psum x2 -> x0, blocking collectives: 79 us -> none  [the longest x1 39.6 us: body(): lax.psum(jnp.stack([inner_product(residual, response), inner_product(resp...]
    slice x47 -> x1, local copies, waits for them, and re-layouts: 44.5 us -> 0.63 us  [body(): return (updated, trial[:, 0])]
    ppermute x24 -> x0, local copies, waits for them, and re-layouts: 38.2 us -> none  [the longest x12 19.1 us: with_halo(): lax.ppermute(lax.slice_in_dim(block, 0, width, axis=dim), axis, backward)]
    reduce_sum x4 -> x0, other arithmetic: 33.1 us -> none  [the longest x2 17.3 us: precondition(): coarse_res = remainder.reshape(blocked).mean(axis=(2, 4, 6))]
    add x10 -> x0, other arithmetic: 15.1 us -> none  [the longest x1 6.45 us: precondition(): return second + WEIGHT * (residual - fine_operator(second)) / FINE_DIAG]
  transfers between devices with their start and end apart: 72 -> 0, of which waited for: 59 -> 0; matrix products, arithmetic and copies ran while one was open for 6% -> 0% of each run, Pallas kernels for 0% -> 0%
where the time goes in v1:
time: 110 us; the launch traced here: 109 us
  Pallas kernels  105 us (95%)
  local copies, waits for them, and re-layouts  3.65 us (3%)
    pallas_call x1, Pallas kernels, body(): pl.pallas_call(call, out_shape=(jax.ShapeDtypeStruct(orbitals.shape, jnp....  105 us
    unnamed x5, local copies, waits for them, and re-layouts  3.03 us

profile of v1, /device:TPU:0, one launch (start us, length us, event | category | flops | bytes accessed | tf_op | source)
XLA Modules:
  0.0 109.4 jit_solution(8578732818504427419)
XLA Ops:
  0.6 0.0 copy-start
  0.6 1.2 %copy-done = f32[16,8,8,256]{3,2,1,0:T(8,128)S(1)} copy-done((f32[16,8,8,256]{3,2,1,0:T(8,128)S(1)}, f32[16,8,8,256]{3,2,1,0:T(8,128)}, u32[]{:S(2)}) %copy-start) | copy-done | bytes 1048600
  1.9 0.0 copy-start.1
  1.9 0.8 copy-done.1
  2.7 105.1 %shard_map.41 = (f32[16,8,8,256]{3,2,1,0:T(8,128)S(1)}, f32[16,128]{1,0:T(8,128)S(1)}) custom-call(f32[16,8,8,256]{3,2,1,0:T(8,128)S(1)} %copy-done, f32[8,8,256]{2,1,0:T(8,128)S(1)} %copy-done.1), custom_call_target="tpu_custom_call" | custom-call | tf_op jit(solution)/shard_map/pallas_call | solution.py:507
  107.8 0.6 slice_reduce_fusion
  108.4 1.0 copy.5
Async XLA Ops:
  0.6 1.2 %copy-start = (f32[16,8,8,256]{3,2,1,0:T(8,128)S(1)}, f32[16,8,8,256]{3,2,1,0:T(8,128)}, u32[]{:S(2)}) copy-start(f32[16,8,8,256]{3,2,1,0:T(8,128)} %refs_0_.1) | copy-start | bytes 3145732
  1.9 0.8 copy-start.1
